TPU v7x, 128 devices: a whole 4x4x4 slice. The times are simulated.
128 devices in a mesh: vocab: 64 (over y, z, x), dp: 2 (over core).
Axes of the slice: x: 4, y: 4, z: 4, core: 2. Of those that a mesh axis runs over, the one named last changes fastest.
Arguments:
- hidden: bfloat16 [2048, 4096], P('dp', 'vocab'), may hold values from -64 to 64
- head_weight: bfloat16 [65536, 4096], P('vocab'), may hold values from -0.28125 to 0.28125
- targets: int32 [2048], P('dp'), may hold values from 0 to 65535
- loss_cot: float32 [2048], P('dp'), may hold values from -40 to 40
Outputs:
- tok_loss: float32 [2048], P('dp')
- hidden_grad: bfloat16 [2048, 4096], P('dp', 'vocab')
- g_factor: float32 [65536, 1024], P(('vocab', 'dp'))
- a_factor: float32 [4096, 4096], P('vocab')
All inputs are finite; a program needn't handle non-finite values.
Results may differ from a plain program's by a relative error of at most 0.0049.
Values may be sent and summed in bfloat16 or wider, within the bound.
No kernel may reach another device: no remote copies, remote signals or barrier semaphores. Data moves between devices by JAX's collectives and lax.ppermute only.
A program may use at most 128 MiB of HBM per device.

v0:
```python
import jax
import jax.numpy as jnp
from jax import lax
from jax.sharding import Mesh
from jax.sharding import PartitionSpec as P

TOK_DEV = 1024
VOCAB = ("vocab_0", "vocab_1", "vocab_2")
VOCAB_DP = ("vocab_0", "vocab_1", "vocab_2", "dp")


def from_everyone(x, axis):
    count = lax.axis_size(axis)
    return lax.all_to_all(jnp.broadcast_to(x[None], (count, *x.shape)), axis, 0, 0, tiled=True)


def gathered_once(x, axis):
    leaves = jax.tree.leaves(x)
    order = sorted(range(len(leaves)), key=lambda k: -leaves[k].size)
    width = (1, *leaves[order[0]].shape)[-1]
    lines = [
        jnp.pad(leaves[k].reshape(-1), (0, -leaves[k].size % width)).reshape(-1, width)
        for k in order
    ]
    both, at, found = (from_everyone(jnp.concatenate(lines), axis), 0, {})
    for k, line in zip(order, lines):
        piece = both[:, at : at + len(line)].reshape(len(both), -1)
        found[k] = piece[:, : leaves[k].size].reshape(-1, *leaves[k].shape)
        at += len(line)
    numbers = iter(range(len(leaves)))
    return jax.tree.map(lambda _: found[next(numbers)], x)


def combined_pairwise(pieces, combine):
    while len(jax.tree.leaves(pieces)[0]) > 1:
        pieces = jax.vmap(combine)(
            *(jax.tree.map(lambda part: part[side::2], pieces) for side in (0, 1))
        )
    return jax.tree.map(lambda part: part[0], pieces)


def merged(x, axis, combine):
    pieces = gathered_once(x, axis)
    return combined_pairwise(pieces, combine)


def cut_along(x, dim, count):
    before, after = (x.shape[:dim], x.shape[dim + 1 :])
    return jnp.moveaxis(x.reshape(*before, count, -1, *after), dim, 0)


def piece_ends(length, count):
    step = length // count
    if step >= 8:
        step -= step % 8
    return [step * k for k in range(1, count)]


def sum_in_order(pieces, axes, order):
    dims = [lax.axis_size(a) for a in axes]
    pieces = pieces.reshape(*dims, *pieces.shape[1:])
    pieces = pieces.transpose(*order, *range(len(axes), pieces.ndim))
    pieces = pieces.reshape(-1, *pieces.shape[len(axes) :])
    for k in order:
        pieces = lax.psum_scatter(pieces, axes[k], scatter_dimension=0, tiled=True)
    return pieces[0]


def spread_scatter(x, axes, dim):
    pieces = cut_along(x, dim, lax.axis_size(axes))
    split_at = max(range(1, max(2, pieces.ndim - 1)), key=lambda d: pieces.shape[d])
    count, done = (len(axes), [])
    for first, piece in enumerate(
        jnp.split(pieces, piece_ends(pieces.shape[split_at], count), axis=split_at)
    ):
        if piece.size:
            order = [(first + k) % count for k in range(count)]
            done.append(sum_in_order(piece, axes, order))
    return jnp.concatenate(done, axis=split_at - 1)


def sent_and_summed(x, axis, dim):
    count = lax.axis_size(axis)
    pieces = lax.all_to_all(cut_along(x, dim, count), axis, 0, 0, tiled=True)
    return jnp.sum(pieces, axis=0)


def over_copies(x, axis):
    everything = from_everyone(x, axis)
    return jnp.sum(everything, axis=0)


def combine(earlier, later):
    top_now = jnp.maximum(earlier[0], later[0])
    summed = earlier[1] * jnp.exp(earlier[0] - top_now) + later[1] * jnp.exp(later[0] - top_now)
    return (top_now, summed, earlier[2] + later[2])


def body(hidden, head_weight, targets, loss_cot):
    vocab_rows, width = head_weight.shape
    piece = lax.all_gather(hidden, VOCAB, axis=1, tiled=True)
    logits = lax.dot_general(
        piece, head_weight, (((1,), (1,)), ((), ())), preferred_element_type=jnp.float32
    )
    a_block = lax.dot_general(
        hidden, piece, (((0,), (0,)), ((), ())), preferred_element_type=jnp.float32
    )
    a_local = a_block
    logits, a_local = (logits, a_local)
    offset = lax.axis_index(VOCAB) * vocab_rows
    onehot = (targets - offset)[:, None] == jnp.arange(vocab_rows, dtype=jnp.int32)[None, :]
    local_top = jnp.max(logits, axis=1)
    local_target = jnp.sum(jnp.where(onehot, logits, jnp.float32(0.0)), axis=1)
    local_scaled = jnp.exp(logits - local_top[:, None])
    local_total = jnp.sum(local_scaled, axis=1)
    row_top, row_total, target_logit = merged(
        (local_top, local_total, local_target), VOCAB, combine
    )
    scaled = local_scaled * jnp.exp(local_top - row_top)[:, None]
    tok_loss = jnp.log(row_total) + row_top - target_logit
    prob = scaled / row_total[:, None]
    out_grad = (loss_cot[:, None] * (prob - onehot.astype(jnp.float32))).astype(jnp.bfloat16)
    partial_grad = jnp.dot(out_grad, head_weight, preferred_element_type=jnp.float32)
    hidden_grad = spread_scatter(partial_grad, VOCAB, 1).astype(jnp.bfloat16)
    g_local = (
        lax.dot_general(
            out_grad, out_grad, (((0,), (0,)), ((), ())), preferred_element_type=jnp.float32
        )
        / TOK_DEV
    )
    g_factor = sent_and_summed(g_local, "dp", 0)
    a_factor = over_copies(a_local / TOK_DEV, "dp")
    return (tok_loss, hidden_grad, g_factor, a_factor)


def solution(mesh):
    finer = Mesh(
        mesh.devices.reshape(4, 4, 4, mesh.shape["dp"]), ("vocab_0", "vocab_1", "vocab_2", "dp")
    )
    return jax.shard_map(
        body,
        mesh=finer,
        in_specs=(P("dp", VOCAB), P(VOCAB, None), P("dp"), P("dp")),
        out_specs=(P("dp"), P("dp", VOCAB), P(VOCAB_DP, None), P(VOCAB, None)),
        check_vma=False,
    )
```

profile of v0, /device:TPU:0, one launch (start us, length us, event | category | flops | bytes accessed | tf_op | source)
XLA Modules:
  0.0 524.4 jit_solution(4430448576788569282)
XLA Ops:
  7.2 0.0 all-gather.2.cloned.1.call-start
  7.2 0.7 all-gather.2.cloned.1.call-update
  7.9 0.0 reduce-scatter.16.cloned.1.call-start
  8.0 0.7 broadcast_subtract_fusion
  8.6 83.1 %all-gather.2.cloned.1.call-done = bf16[1024,4096]{0,1:T(8,128)(2,1)} async-done(((bf16[1024,64]{0,1:T(8,128)(2,1)}), bf16[1024,4096]{0,1:T(8,128)(2,1)}) %all-gather.2.cloned.1.call-update) | async-done | bytes 8388624 | tf_op jit(solution)/shard_map/all_gather | solution.py:101
  91.7 12.9 %fusion.5 = (f32[1024]{0:T(1024)S(1)}, f32[1024,1024]{0,1:T(8,128)S(1)}) fusion(bf16[1024,4096]{1,0:T(8,128)(2,1)} %param.5, bf16[1024,4096]{0,1:T(8,128)(2,1)} %all-gather.2.cloned.1.call-done), kind=kOutput, calls=%fused_computation.31 | convolution fusion | flops 8590982144 | bytes 20975616 | tf_op jit(solution)/shard_map/dot_general | solution.py:102
  104.6 1.1 fusion
  105.8 0.2 broadcast_in_dim.9
  106.0 27.2 %all_to_all.15 = f32[64,3,1024]{2,1,0:T(4,128)S(1)} all-to-all(f32[64,3,1024]{2,1,0:T(4,128)S(1)} %broadcast_in_dim.9), channel_id=1, replica_groups=mesh['vocab_0'=4,'vocab_1'=4,'vocab_2'=4,'dp'=2] {'vocab_0','vocab_1','v..., dimensions={0} | all-to-all | bytes 1572864 | tf_op jit(solution)/shard_map/all_to_all | solution.py:14
  133.2 0.5 fusion.4
  133.9 0.1 copy_bitcast_fusion
  134.1 0.1 multiply_add_fusion
  135.1 0.6 subtract_exponential_fusion.1
  135.8 16.8 %fusion.2 = f32[1024,4096]{0,1:T(8,128)} fusion(bf16[1024,4096]{1,0:T(8,128)(2,1)} %param.5, f32[1024,1024]{0,1:T(8,128)} %copy-done, f32[1024]{0:T(1024)S(1)} %bitcast.48, f32[1024]{0:T(1024)S(1)} %get-tuple-element.23, f32[1024]{0:T(1024)S(1)} %copy-done.2, s32[1024]{0:T(1024)S(1)} %broadcast_subtract_fusion, f32[1024]{0:T(1024)S(1)} %get-tuple-element.25), kind=kOutput, calls=%fused_computation.28 | convolution fusion | flops 8598323200 | bytes 29380608 | tf_op jit(solution)/shard_map/dot_general | solution.py:123
  152.6 11.7 %fusion.3 = (f32[64,336,64]{1,2,0:T(8,128)}, f32[64,336,64]{1,2,0:T(8,128)}) fusion(f32[64,1024,64]{1,2,0:T(8,128)} %bitcast.40), kind=kLoop, calls=%fused_computation.29 | loop fusion | bytes 22020096 | tf_op jit(solution)/shard_map/split | solution.py:74
  164.2 6.2 %copy.18 = f32[4,4,4,336,64]{3,4,2,1,0:T(8,128)} copy(f32[4,4,4,336,64]{3,4,1,0,2:T(8,128)} %bitcast.39) | data formatting | bytes 11010048 | tf_op jit(solution)/shard_map/transpose | solution.py:62
  170.5 0.0 reduce-scatter.16.cloned.1.call-update
  170.5 0.0 reduce-scatter.10.cloned.1.call-start
  170.5 0.7 reduce-scatter.10.cloned.1.call-update
  171.2 0.0 reduce-scatter.22.cloned.1.call-start
  171.3 4.5 split.14
  175.8 3.1 copy.19
  178.8 0.0 reduce-scatter.18.cloned.1.call-start
  178.9 51.5 %reduce-scatter.16.cloned.1.call-done = f32[16,336,64]{1,2,0:T(8,128)} async-done(((f32[64,336,64]{1,2,0:T(8,128)}), f32[16,336,64]{1,2,0:T(8,128)}) %reduce-scatter.16.cloned.1.call-update) | async-done | bytes 1376272 | tf_op jit(solution)/shard_map/reduce_scatter | solution.py:65
  230.4 0.0 reduce-scatter.12.cloned.1.call-start
  230.4 65.9 %reduce-scatter.10.cloned.1.call-done = f32[16,336,64]{1,2,0:T(8,128)} async-done(((f32[64,336,64]{1,2,0:T(8,128)}), f32[16,336,64]{1,2,0:T(8,128)}) %reduce-scatter.10.cloned.1.call-update) | async-done | bytes 1376272 | tf_op jit(solution)/shard_map/reduce_scatter | solution.py:65
  296.4 0.0 reduce-scatter.24.cloned.1.call-start
  296.4 65.9 %reduce-scatter.22.cloned.1.call-done = f32[16,352,64]{1,2,0:T(8,128)} async-done(((f32[64,352,64]{1,2,0:T(8,128)}), f32[16,352,64]{1,2,0:T(8,128)}) %reduce-scatter.22.cloned.1.call-update) | async-done | bytes 1441808 | tf_op jit(solution)/shard_map/reduce_scatter | solution.py:65
  362.4 0.0 reduce-scatter.20.cloned.1.call-start
  362.4 27.6 %reduce-scatter.18.cloned.1.call-done = f32[4,336,64]{1,2,0:T(8,128)} async-done(((f32[16,336,64]{1,2,0:T(8,128)}), f32[4,336,64]{1,2,0:T(8,128)}) %reduce-scatter.18.cloned.1.call-update) | async-done | bytes 344080 | tf_op jit(solution)/shard_map/reduce_scatter | solution.py:65
  390.0 0.0 reduce-scatter.14.cloned.1.call-start
  390.1 27.9 %reduce-scatter.12.cloned.1.call-done = f32[4,336,64]{1,2,0:T(8,128)} async-done(((f32[16,336,64]{1,2,0:T(8,128)}), f32[4,336,64]{1,2,0:T(8,128)}) %reduce-scatter.12.cloned.1.call-update) | async-done | bytes 344080 | tf_op jit(solution)/shard_map/reduce_scatter | solution.py:65
  418.0 0.3 reduce-scatter.26.cloned.1.call-start
  418.2 6.0 %convolution_multiply_fusion = f32[64,4096]{1,0:T(8,128)S(1)} fusion(bf16[1024,64]{0,1:T(8,128)(2,1)S(1)} %copy-done.1, bf16[1024,4096]{0,1:T(8,128)(2,1)} %all-gather.2.cloned.1.call-done), kind=kOutput, calls=%fused_computation | convolution fusion | flops 537133056 | bytes 9568256 | tf_op jit(solution)/shard_map/dot_general | solution.py:105
  424.3 0.2 broadcast_in_dim.10
  424.5 5.4 %all_to_all.16 = f32[2,64,4096]{2,1,0:T(8,128)S(1)} all-to-all(f32[2,64,4096]{2,1,0:T(8,128)S(1)} %broadcast_in_dim.10), channel_id=1, replica_groups=mesh['vocab_0'=4,'vocab_1'=4,'vocab_2'=4,'dp'=2] {'dp'}, dimensions={0} | all-to-all | bytes 4194304 | tf_op jit(solution)/shard_map/all_to_all | solution.py:14
  429.9 1.2 reduce_sum.39
  431.1 14.6 %reduce-scatter.24.cloned.1.call-done = f32[4,352,64]{1,2,0:T(8,128)} async-done(((f32[16,352,64]{1,2,0:T(8,128)}), f32[4,352,64]{1,2,0:T(8,128)}) %reduce-scatter.24.cloned.1.call-update) | async-done | bytes 360464 | tf_op jit(solution)/shard_map/reduce_scatter | solution.py:65
  445.8 7.7 %convolution_multiply_fusion.1 = f32[1024,1024]{1,0:T(8,128)S(1)} fusion(f32[1024,1024]{0,1:T(8,128)} %copy-done, f32[1024]{0:T(1024)S(1)} %bitcast.49, f32[1024]{0:T(1024)S(1)} %get-tuple-element.23, f32[1024]{0:T(1024)S(1)} %copy-done.2, s32[1024]{0:T(1024)S(1)} %broadcast_subtract_fusion, f32[1024]{0:T(1024)S(1)} %get-tuple-element.25), kind=kOutput, calls=%fused_computation.6 | convolution fusion | flops 2156920832 | bytes 8409088 | tf_op jit(solution)/shard_map/dot_general | solution.py:126
  453.5 8.2 %all_to_all.17 = f32[2,512,1024]{2,1,0:T(8,128)} all-to-all(f32[2,512,1024]{2,1,0:T(8,128)S(1)} %bitcast.42), channel_id=1, replica_groups=mesh['vocab_0'=4,'vocab_1'=4,'vocab_2'=4,'dp'=2] {'dp'}, dimensions={0} | all-to-all | bytes 8388608 | tf_op jit(solution)/shard_map/all_to_all | solution.py:84
  461.6 4.1 reduce_sum.38
  465.8 3.4 reduce-scatter.20.cloned.1.call-done
  469.1 0.9 convert_bitcast_fusion.1
  470.0 22.4 %reduce-scatter.14.cloned.1.call-done = f32[1,336,64]{1,2,0:T(8,128)} async-done(((f32[4,336,64]{1,2,0:T(8,128)}), f32[1,336,64]{1,2,0:T(8,128)}) %reduce-scatter.14.cloned.1.call-update) | async-done | bytes 86032 | tf_op jit(solution)/shard_map/reduce_scatter | solution.py:65
  492.5 0.9 convert_bitcast_fusion.2
  493.4 22.6 %reduce-scatter.26.cloned.1.call-done = f32[1,352,64]{1,2,0:T(8,128)} async-done(((f32[4,352,64]{1,2,0:T(8,128)}), f32[1,352,64]{1,2,0:T(8,128)}) %reduce-scatter.26.cloned.1.call-update) | async-done | bytes 90128 | tf_op jit(solution)/shard_map/reduce_scatter | solution.py:65
  515.9 0.9 convert_bitcast_fusion
  516.8 0.8 pad_maximum_fusion
  (56 shorter events, 1.2 us)
Async XLA Ops:
  7.2 84.6 %all-gather.2.cloned.1.call-start = ((), (), s32[]{:S(2)}) async-start(), calls=%async_computation.12 | async-start | bytes 8519680 | tf_op jit(solution)/shard_map/all_gather | solution.py:101
  7.9 222.5 %reduce-scatter.16.cloned.1.call-start = ((), (), s32[]{:S(2)}) async-start(), calls=%async_computation.16 | async-start | bytes 7864320 | tf_op jit(solution)/shard_map/reduce_scatter | solution.py:65
  104.6 29.1 %copy-start = (f32[1024,1024]{0,1:T(8,128)}, f32[1024,1024]{0,1:T(8,128)S(1)}, u32[]{:S(2)}) copy-start(f32[1024,1024]{0,1:T(8,128)S(1)} %get-tuple-element.26) | copy-start | bytes 12582916
  133.2 2.6 copy-start.2
  170.5 125.9 %reduce-scatter.10.cloned.1.call-start = ((), (), s32[]{:S(2)}) async-start(), calls=%async_computation.13 | async-start | bytes 7864320 | tf_op jit(solution)/shard_map/reduce_scatter | solution.py:65
  171.2 191.1 %reduce-scatter.22.cloned.1.call-start = ((), (), s32[]{:S(2)}) async-start(), calls=%async_computation.19 | async-start | bytes 7864320 | tf_op jit(solution)/shard_map/reduce_scatter | solution.py:65
  178.8 239.4 %copy-start.1 = (bf16[1024,64]{0,1:T(8,128)(2,1)S(1)}, bf16[1024,64]{0,1:T(8,128)(2,1)}, u32[]{:S(2)}) copy-start(bf16[1024,64]{0,1:T(8,128)(2,1)} %param.4) | copy-start | bytes 393220
  178.8 211.2 %reduce-scatter.18.cloned.1.call-start = ((), (), s32[]{:S(2)}) async-start(), calls=%async_computation.17 | async-start | bytes 1966080 | tf_op jit(solution)/shard_map/reduce_scatter | solution.py:65
  230.4 187.6 %reduce-scatter.12.cloned.1.call-start = ((), (), s32[]{:S(2)}) async-start(), calls=%async_computation.14 | async-start | bytes 1966080 | tf_op jit(solution)/shard_map/reduce_scatter | solution.py:65
  296.4 149.3 %reduce-scatter.24.cloned.1.call-start = ((), (), s32[]{:S(2)}) async-start(), calls=%async_computation.20 | async-start | bytes 1966080 | tf_op jit(solution)/shard_map/reduce_scatter | solution.py:65
  362.4 106.8 %reduce-scatter.20.cloned.1.call-start = ((), (), s32[]{:S(2)}) async-start(), calls=%async_computation.18 | async-start | bytes 491520 | tf_op jit(solution)/shard_map/reduce_scatter | solution.py:65
  390.0 102.4 %reduce-scatter.14.cloned.1.call-start = ((), (), s32[]{:S(2)}) async-start(), calls=%async_computation.15 | async-start | bytes 491520 | tf_op jit(solution)/shard_map/reduce_scatter | solution.py:65
  418.0 98.0 %reduce-scatter.26.cloned.1.call-start = ((), (), s32[]{:S(2)}) async-start(), calls=%async_computation.21 | async-start | bytes 491520 | tf_op jit(solution)/shard_map/reduce_scatter | solution.py:65
Sparse Core Ops, SparseCore 0:
  10.8 80.8 all-gather.1
  170.6 59.6 reduce-scatter.15
  232.8 63.5 reduce-scatter.9
  298.6 63.6 reduce-scatter.21
  364.6 25.3 reduce-scatter.17
  392.3 25.6 reduce-scatter.11
  420.3 25.3 reduce-scatter.23
  448.1 20.9 reduce-scatter.19
  471.5 20.8 reduce-scatter.13
  494.7 21.1 reduce-scatter.25
where the time goes:
time: 525 us; the launch traced here: 524 us
  waiting for transfers between devices  386 us (74%)
  matrix products  43.4 us (8%)
  blocking collectives  40.7 us (8%)
  local copies, waits for them, and re-layouts  27.4 us (5%)
  between operations  14.4 us (3%)
  other arithmetic  11.4 us (2%)
    reduce_scatter x9, waiting for transfers between devices, sum_in_order(): pieces = lax.psum_scatter(pieces, axes[k], scatter_dimension=0, tiled=True)  302 us
    all_gather x1, waiting for transfers between devices, body(): piece = lax.all_gather(hidden, VOCAB, axis=1, tiled=True)  83.1 us
    all_to_all x2, blocking collectives, from_everyone(): lax.all_to_all(jnp.broadcast_to(x[None], (count, *x.shape)), axis, 0, 0,...  32.6 us
    dot_general x1, matrix products, body(): jnp.dot(out_grad, head_weight, preferred_element_type=jnp.float32)  16.8 us
    split x2, local copies, waits for them, and re-layouts, spread_scatter(): jnp.split(pieces, piece_ends(pieces.shape[split_at], count), axis=split_at)  16.1 us
    dot_general x1, matrix products, body(): lax.dot_general(piece, head_weight, (((1,), (1,)), ((), ())), preferred_e...  12.9 us
  transfers between devices with their start and end apart: 10, of which 10 were waited for; matrix products, arithmetic and copies ran while one was open for 6% of the time, Pallas kernels for 0%

commit v1 on v0

v1 whole, which is shorter than its diff:
```python
import jax
import jax.numpy as jnp
import numpy as np
from jax import lax
from jax.sharding import Mesh
from jax.sharding import PartitionSpec as P

TOK_DEV = 1024
VOCAB = ("vocab_0", "vocab_1", "vocab_2")
ALL = ("vocab_0", "vocab_1", "vocab_2", "dp")

ORDER = (((0, 1), (2, 3)), ((0, 3), (1, 2)))
SMALL = (((0, 1), (2, 3)), ((0, 3), (1, 2)))
LARGE = (((1, 2), (0, 3)), ((0, 1), (3, 2)))


def cubes(pairs):
    groups = []
    for core in (0, 1):
        for a in pairs[core]:
            for b in pairs[core]:
                for c in pairs[core]:
                    groups.append(
                        [((y * 4 + z) * 4 + x) * 2 + core for y in a for z in b for x in c]
                    )
    return groups


def chip_order(core):
    o = ORDER[core]
    bits = (0, 1)
    return [
        (o[jy][iy] * 4 + o[jz][iz]) * 4 + o[jx][ix]
        for jy in bits for jz in bits for jx in bits
        for iy in bits for iz in bits for ix in bits
    ]


SMALL_CUBES = cubes(SMALL)
LARGE_CUBES = cubes(LARGE)
CHIPS = np.array([chip_order(0), chip_order(1)], np.int32)
PLACES = np.argsort(CHIPS, axis=1).astype(np.int32)
SWAP = [(0, 1), (1, 0)]


def exchanged(x, groups):
    return lax.all_to_all(x, ALL, 0, 0, axis_index_groups=groups, tiled=True)


def to_cube(x, groups):
    return exchanged(jnp.broadcast_to(x[None], (8, *x.shape)), groups)


def body(hidden, head_weight, targets, loss_cot):
    vocab_rows, width = head_weight.shape
    own = hidden.T
    feats, tokens = own.shape
    core = lax.axis_index("dp")
    some = to_cube(own, SMALL_CUBES).reshape(8 * feats, tokens)
    gathered = to_cube(some, LARGE_CUBES).reshape(64, feats, tokens)
    everything = jnp.take(gathered, jnp.asarray(PLACES)[core], axis=0).reshape(width, tokens)
    logits = jnp.dot(head_weight, everything, preferred_element_type=jnp.float32)
    a_part = lax.dot_general(
        own, everything, (((1,), (1,)), ((), ())), preferred_element_type=jnp.float32
    )
    offset = lax.axis_index(VOCAB) * vocab_rows
    onehot = jnp.arange(vocab_rows, dtype=jnp.int32)[:, None] == (targets - offset)[None, :]
    local_top = jnp.max(logits, axis=0)
    local_target = jnp.sum(jnp.where(onehot, logits, jnp.float32(0.0)), axis=0)
    local_total = jnp.sum(jnp.exp(logits - local_top[None, :]), axis=0)
    stats = jnp.stack([local_top, local_total, local_target])
    stats = lax.all_to_all(
        jnp.broadcast_to(stats.reshape(1, 24, 128), (64, 24, 128)), VOCAB, 0, 0, tiled=True
    ).reshape(64, 3, tokens)
    row_top = jnp.max(stats[:, 0], axis=0)
    row_total = jnp.sum(stats[:, 1] * jnp.exp(stats[:, 0] - row_top[None, :]), axis=0)
    target_logit = jnp.sum(stats[:, 2], axis=0)
    tok_loss = jnp.log(row_total) + row_top - target_logit
    prob = jnp.exp(logits - row_top[None, :]) / row_total[None, :]
    out_grad = (loss_cot[None, :] * (prob - onehot.astype(jnp.float32))).astype(jnp.bfloat16)
    part = lax.dot_general(
        head_weight, out_grad, (((0,), (0,)), ((), ())), preferred_element_type=jnp.float32
    ).astype(jnp.bfloat16)
    part = jnp.take(part.reshape(64, feats, tokens), jnp.asarray(CHIPS)[core], axis=0)
    part = exchanged(part.reshape(8, 8 * feats, tokens), LARGE_CUBES)
    part = jnp.sum(part.astype(jnp.float32), axis=0).astype(jnp.bfloat16)
    part = exchanged(part.reshape(8, feats, tokens), SMALL_CUBES)
    hidden_grad = jnp.sum(part.astype(jnp.float32), axis=0).astype(jnp.bfloat16).T
    other = lax.ppermute(out_grad, "dp", SWAP)
    rows = vocab_rows // 2

    def gram(x):
        mine = lax.dynamic_slice_in_dim(x, core * rows, rows, 0)
        return lax.dot_general(mine, x, (((1,), (1,)), ((), ())), preferred_element_type=jnp.float32)

    g_factor = (gram(out_grad) + gram(other)) / TOK_DEV
    a_factor = (a_part + lax.ppermute(a_part, "dp", SWAP)) / TOK_DEV
    return (tok_loss, hidden_grad, g_factor, a_factor)


def solution(mesh):
    finer = Mesh(mesh.devices.reshape(4, 4, 4, mesh.shape["dp"]), ALL)
    return jax.shard_map(
        body,
        mesh=finer,
        in_specs=(P("dp", VOCAB), P(VOCAB, None), P("dp"), P("dp")),
        out_specs=(P("dp"), P("dp", VOCAB), P(ALL, None), P(VOCAB, None)),
        check_vma=False,
    )
```

time: 525 us -> 285 us (0.54)
  waiting for transfers between devices: 386 us -> 120 us
  starting transfers between devices: 0.61 us -> 32.1 us
  blocking collectives: 40.7 us -> 16.2 us
  other arithmetic: 11.4 us -> 30.8 us
  between operations: 14.4 us -> 0.8 us
  local copies, waits for them, and re-layouts: 27.4 us -> 38.3 us
    reduce_scatter x9 -> x0, waiting for transfers between devices: 302 us -> none  [sum_in_order(): pieces = lax.psum_scatter(pieces, axes[k], scatter_dimension=0, tiled=True)]
    all_to_all x0 -> x4, waiting for transfers between devices: none -> 120 us  [the longest x3 104 us: exchanged(): return lax.all_to_all(x, ALL, 0, 0, axis_index_groups=groups, tiled=True)]
    all_gather x1 -> x0, waiting for transfers between devices: 83.1 us -> none  [body(): piece = lax.all_gather(hidden, VOCAB, axis=1, tiled=True)]
    all_to_all x0 -> x4, starting transfers between devices: none -> 31.3 us  [the longest x3 18.4 us: exchanged(): return lax.all_to_all(x, ALL, 0, 0, axis_index_groups=groups, tiled=True)]
    all_to_all x3 -> x1, blocking collectives: 40.7 us -> 16.2 us  [exchanged(): return lax.all_to_all(x, ALL, 0, 0, axis_index_groups=groups, tiled=True)]
    gather x0 -> x2, local copies, waits for them, and re-layouts: none -> 17.8 us  [the longest x1 8.91 us: body(): jnp.take(part.reshape(64, feats, tokens), jnp.asarray(CHIPS)[core], axis=0)]
    split x2 -> x0, local copies, waits for them, and re-layouts: 16.1 us -> none  [spread_scatter(): jnp.split(pieces, piece_ends(pieces.shape[split_at], count), axis=split_at)]
    select_n x0 -> x2, other arithmetic: none -> 14.9 us  [the longest x1 7.47 us: body(): jnp.take(part.reshape(64, feats, tokens), jnp.asarray(CHIPS)[core], axis=0)]
  transfers between devices with their start and end apart: 10 -> 6, of which waited for: 10 -> 4; matrix products, arithmetic and copies ran while one was open for 6% -> 9% of each run, Pallas kernels for 0% -> 0%
where the time goes in v1:
time: 285 us; the launch traced here: 282 us
  waiting for transfers between devices  120 us (42%)
  matrix products  43.7 us (15%)
  local copies, waits for them, and re-layouts  38.3 us (13%)
  starting transfers between devices  32.1 us (11%)
  other arithmetic  30.8 us (11%)
  blocking collectives  16.2 us (6%)
    all_to_all x3, waiting for transfers between devices, exchanged(): return lax.all_to_all(x, ALL, 0, 0, axis_index_groups=groups, tiled=True)  104 us
    all_to_all x3, starting transfers between devices, exchanged(): return lax.all_to_all(x, ALL, 0, 0, axis_index_groups=groups, tiled=True)  18.4 us
    all_to_all x1, waiting for transfers between devices, body(): lax.all_to_all(jnp.broadcast_to(stats.reshape(1, 24, 128), (64, 24, 128))...  16.4 us
    all_to_all x1, blocking collectives, exchanged(): return lax.all_to_all(x, ALL, 0, 0, axis_index_groups=groups, tiled=True)  16.2 us
    dot_general x1, matrix products, body(): lax.dot_general(head_weight, out_grad, (((0,), (0,)), ((), ())), preferre...  14.8 us
    all_to_all x1, starting transfers between devices, body(): lax.all_to_all(jnp.broadcast_to(stats.reshape(1, 24, 128), (64, 24, 128))...  12.9 us
    dot_general x1, matrix products, body(): jnp.dot(head_weight, everything, preferred_element_type=jnp.float32)  12.9 us
    convert_element_type x1, local copies, waits for them, and re-layouts, body(): part = lax.dot_general(head_weight, out_grad, (((0,), (0,)), ((), ())), p...  12 us
  transfers between devices with their start and end apart: 6, of which 4 were waited for; matrix products, arithmetic and copies ran while one was open for 9% of the time, Pallas kernels for 0%

profile of v1, /device:TPU:0, one launch (start us, length us, event | category | flops | bytes accessed | tf_op | source)
XLA Modules:
  0.0 282.2 jit_solution(407535265369571170)
XLA Ops:
  0.6 1.0 broadcast_in_dim.23
  1.7 16.2 %all_to_all.25 = bf16[8,64,1024]{2,1,0:T(8,128)(2,1)S(1)} all-to-all(bf16[8,64,1024]{2,1,0:T(8,128)(2,1)S(1)} %broadcast_in_dim.23), channel_id=1, replica_groups={{0,2,8,10,32,34,40,42},{4,6,12,14,36,38,44,46},{16,18,24,26,48,50,56,58..., dimensions={0} | all-to-all | bytes 2097152 | tf_op jit(solution)/shard_map/all_to_all | solution.py:47
  17.9 4.3 %broadcast_in_dim.42 = bf16[8,512,1024]{2,1,0:T(8,128)(2,1)} broadcast(bf16[512,1024]{1,0:T(8,128)(2,1)S(1)} %bitcast.69), dimensions={1,2} | broadcast | bytes 9437184 | tf_op jit(solution)/shard_map/broadcast_in_dim | solution.py:51
  22.2 0.0 copy-start.5
  22.2 0.0 copy-start.3
  22.2 6.8 %all-to-all-start.1 = ((bf16[8,512,1024]{2,1,0:T(8,128)(2,1)}), bf16[8,512,1024]{2,1,0:T(8,128)(2,1)}, u32[]{:S(2)}, u32[]{:S(2)}) async-start(bf16[8,512,1024]{2,1,0:T(8,128)(2,1)} %broadcast_in_dim.42), calls=%async_computation.1 | async-start | bytes 16777216 | tf_op jit(solution)/shard_map/all_to_all | solution.py:47
  29.0 0.0 copy-done.5
  29.0 0.0 copy-done.3
  29.0 55.6 %all-to-all-done.1 = bf16[8,512,1024]{2,1,0:T(8,128)(2,1)} async-done(((bf16[8,512,1024]{2,1,0:T(8,128)(2,1)}), bf16[8,512,1024]{2,1,0:T(8,128)(2,1)}, u32[]{:S(2)}, u32[]{:S(2)}) %all-to-all-start.1) | async-done | bytes 8388640 | tf_op jit(solution)/shard_map/all_to_all | solution.py:47
  84.7 8.9 %gather_fusion = bf16[64,64,1024]{2,1,0:T(8,128)(2,1)} fusion(bf16[64,64,1024]{2,1,0:T(8,128)(2,1)} %bitcast.3, s32[1024]{0:T(1024)S(1)} %pad_clamp_fusion.1), kind=kCustom, calls=%fused_computation.clone | custom fusion | bytes 16777472 | tf_op jit(solution)/shard_map/jit(_take)/gather | solution.py:61
  93.6 7.5 %broadcast_select_fusion.1 = bf16[64,64,1024]{2,1,0:T(8,128)(2,1)} fusion(bf16[64,64,1024]{2,1,0:T(8,128)(2,1)} %gather_fusion, pred[64]{0:T(512)(128)(4,1)S(1)} %get-tuple-element.11), kind=kLoop, calls=%fused_computation.4 | loop fusion | flops 4194304 | bytes 16777280 | tf_op jit(solution)/shard_map/jit(_take)/select_n | solution.py:61
  101.0 12.9 %fusion.18 = (f32[1024]{0:T(1024)S(1)}, f32[1024,1024]{0,1:T(8,128)S(1)}) fusion(bf16[1024,4096]{1,0:T(8,128)(2,1)} %param.9, bf16[4096,1024]{1,0:T(8,128)(2,1)} %bitcast.65), kind=kOutput, calls=%fused_computation.45 | convolution fusion | flops 8590982144 | bytes 20975616 | tf_op jit(solution)/shard_map/dot_general | solution.py:62
  113.9 0.0 copy-start
  113.9 0.0 copy-start.4
  113.9 1.9 copy-done
  115.8 0.0 copy-start.2
  115.8 1.1 fusion.1
  117.0 0.9 broadcast_in_dim.45
  117.9 12.9 %all-to-all-start.2 = ((f32[64,24,128]{2,1,0:T(8,128)}), f32[64,24,128]{2,1,0:T(8,128)S(1)}, u32[]{:S(2)}, u32[]{:S(2)}) async-start(f32[64,24,128]{2,1,0:T(8,128)} %broadcast_in_dim.45), calls=%async_computation.2 | async-start | bytes 1572864 | tf_op jit(solution)/shard_map/all_to_all | solution.py:72
  130.8 0.0 copy-done.4
  130.8 16.4 %all-to-all-done.2 = f32[64,24,128]{2,1,0:T(8,128)S(1)} async-done(((f32[64,24,128]{2,1,0:T(8,128)}), f32[64,24,128]{2,1,0:T(8,128)S(1)}, u32[]{:S(2)}, u32[]{:S(2)}) %all-to-all-start.2) | async-done | bytes 786464 | tf_op jit(solution)/shard_map/all_to_all | solution.py:72
  147.2 0.3 reshape.42
  147.5 0.6 slice_reduce_fusion.1
  148.2 0.1 fusion.12
  148.3 0.0 copy-done.2
  148.3 4.8 %fusion.7 = bf16[1024,1024]{1,0:T(8,128)(2,1)} fusion(f32[1024,1024]{0,1:T(8,128)} %copy-done, f32[1024]{0:T(1024)S(1)} %fusion.12, f32[1024]{0:T(1024)S(1)} %get-tuple-element.7, f32[1024]{0:T(1024)S(1)} %copy-done.2, s32[1024]{0:T(1024)S(1)} %broadcast_subtract_fusion), kind=kLoop, calls=%fused_computation.17 | loop fusion | flops 7340032 | bytes 6307840 | tf_op jit(solution)/shard_map/convert_element_type | solution.py:80
  153.1 14.8 %convert_bitcast_fusion = bf16[4096,1024]{0,1:T(8,128)(2,1)} fusion(bf16[1024,1024]{1,0:T(8,128)(2,1)} %fusion.7, bf16[1024,4096]{1,0:T(8,128)(2,1)} %param.9), kind=kOutput, calls=%fused_computation.2 | convolution fusion | flops 8594128896 | bytes 18874368 | tf_op jit(solution)/shard_map/dot_general | solution.py:81
  167.9 12.0 %copy.14 = bf16[4096,1024]{1,0:T(8,128)(2,1)} copy(bf16[4096,1024]{0,1:T(8,128)(2,1)} %convert_bitcast_fusion) | data formatting | bytes 16777216 | tf_op jit(solution)/shard_map/convert_element_type | solution.py:83
  179.9 8.9 %gather_fusion.1 = bf16[64,64,1024]{2,1,0:T(8,128)(2,1)} fusion(bf16[64,64,1024]{2,1,0:T(8,128)(2,1)} %bitcast.68, s32[1024]{0:T(1024)S(1)} %pad_clamp_fusion), kind=kCustom, calls=%fused_computation.1.clone | custom fusion | bytes 16777472 | tf_op jit(solution)/shard_map/jit(_take)/gather | solution.py:84
  188.8 7.5 %broadcast_select_fusion = bf16[64,64,1024]{2,1,0:T(8,128)(2,1)} fusion(bf16[64,64,1024]{2,1,0:T(8,128)(2,1)} %gather_fusion.1, pred[64]{0:T(512)(128)(4,1)S(1)} %get-tuple-element.9), kind=kLoop, calls=%fused_computation.3 | loop fusion | flops 4194304 | bytes 16777280 | tf_op jit(solution)/shard_map/jit(_take)/select_n | solution.py:84
  196.3 0.0 copy-start.1
  196.3 5.1 %all-to-all-start.3 = ((bf16[8,512,1024]{2,1,0:T(8,128)(2,1)}), bf16[8,512,1024]{2,1,0:T(8,128)(2,1)}, u32[]{:S(2)}, u32[]{:S(2)}) async-start(bf16[8,512,1024]{2,1,0:T(8,128)(2,1)} %bitcast.67), calls=%async_computation.3 | async-start | bytes 16777216 | tf_op jit(solution)/shard_map/all_to_all | solution.py:47
  201.4 0.1 collective-permute-start
  201.5 0.0 copy-done.1
  201.5 6.0 %convolution_bitcast_fusion = f32[64,4096]{1,0:T(8,128)S(1)} fusion(bf16[4096,1024]{1,0:T(8,128)(2,1)} %bitcast.66, bf16[1024,64]{0,1:T(8,128)(2,1)S(1)} %copy-done.1), kind=kOutput, calls=%fused_computation.5 | convolution fusion | flops 536870912 | bytes 9568256 | tf_op jit(solution)/shard_map/dot_general | solution.py:63
  207.5 0.8 collective-permute-start.1
  208.3 0.6 add_subtract_fusion
  208.9 4.6 %fusion.9 = f32[512,1024]{1,0:T(8,128)} fusion(bf16[1024,1024]{1,0:T(8,128)(2,1)} %fusion.7, s32[]{:T(128)S(6)} %select_n.21), kind=kOutput, calls=%fused_computation.21 | convolution fusion | flops 1073741824 | bytes 5242884 | tf_op jit(solution)/shard_map/dot_general | solution.py:94
  213.5 43.5 %all-to-all-done.3 = bf16[8,512,1024]{2,1,0:T(8,128)(2,1)} async-done(((bf16[8,512,1024]{2,1,0:T(8,128)(2,1)}), bf16[8,512,1024]{2,1,0:T(8,128)(2,1)}, u32[]{:S(2)}, u32[]{:S(2)}) %all-to-all-start.3) | async-done | bytes 8388640 | tf_op jit(solution)/shard_map/all_to_all | solution.py:47
  256.9 6.7 %reduce_sum.64 = bf16[512,1024]{1,0:T(8,128)(2,1)} reduce(bf16[8,512,1024]{2,1,0:T(8,128)(2,1)} %all-to-all-done.3, bf16[]{:T(256)} %constant.50.clone.1), dimensions={0}, to_apply=%region_6.8 | reduce | flops 3670016 | bytes 9437186 | tf_op jit(solution)/shard_map/reduce_sum | solution.py:86
  263.6 6.5 %all-to-all-start.4 = ((bf16[8,64,1024]{2,1,0:T(8,128)(2,1)}), bf16[8,64,1024]{2,1,0:T(8,128)(2,1)S(1)}, u32[]{:S(2)}, u32[]{:S(2)}) async-start(bf16[8,64,1024]{2,1,0:T(8,128)(2,1)} %bitcast.14), calls=%async_computation.4 | async-start | bytes 2097152 | tf_op jit(solution)/shard_map/all_to_all | solution.py:47
  270.1 0.0 collective-permute-done.1
  270.1 1.1 add_multiply_fusion.1
  271.2 0.0 collective-permute-done
  271.2 5.3 %add_multiply_fusion = f32[512,1024]{1,0:T(8,128)} fusion(f32[512,1024]{1,0:T(8,128)} %fusion.9, bf16[1024,1024]{1,0:T(8,128)(2,1)} %collective-permute-done, s32[]{:T(128)S(6)} %select_n.21), kind=kOutput, calls=%fused_computation.18 | convolution fusion | flops 1074790400 | bytes 7340036 | tf_op jit(solution)/shard_map/dot_general | solution.py:94
  276.6 4.8 %all-to-all-done.4 = bf16[8,64,1024]{2,1,0:T(8,128)(2,1)S(1)} async-done(((bf16[8,64,1024]{2,1,0:T(8,128)(2,1)}), bf16[8,64,1024]{2,1,0:T(8,128)(2,1)S(1)}, u32[]{:S(2)}, u32[]{:S(2)}) %all-to-all-start.4) | async-done | bytes 1048608 | tf_op jit(solution)/shard_map/all_to_all | solution.py:47
  281.4 0.8 reduce_sum.65
  (7 shorter events, 0.1 us)
Async XLA Ops:
  22.2 6.8 %copy-start.5 = (s32[2,64]{1,0:T(2,128)S(1)}, s32[2,64]{1,0:T(2,128)}, u32[]{:S(2)}) copy-start(s32[2,64]{1,0:T(2,128)} %constant.53.clone) | copy-start | bytes 1540
  22.2 6.8 %copy-start.3 = (s32[1024]{0:T(1024)S(1)}, s32[1024]{0:T(1024)}, u32[]{:S(2)}) copy-start(s32[1024]{0:T(1024)} %param.10) | copy-start | bytes 12292
  22.2 62.5 %all-to-all-start.1 = ((bf16[8,512,1024]{2,1,0:T(8,128)(2,1)}), bf16[8,512,1024]{2,1,0:T(8,128)(2,1)}, u32[]{:S(2)}, u32[]{:S(2)}) async-start(bf16[8,512,1024]{2,1,0:T(8,128)(2,1)} %broadcast_in_dim.42), calls=%async_computation.1 | async-start | bytes 16777216 | tf_op jit(solution)/shard_map/all_to_all | solution.py:47
  113.9 1.9 copy-start
  113.9 16.9 %copy-start.4 = (s32[2,64]{1,0:T(2,128)S(1)}, s32[2,64]{1,0:T(2,128)}, u32[]{:S(2)}) copy-start(s32[2,64]{1,0:T(2,128)} %constant.54.clone) | copy-start | bytes 1540
  115.8 32.5 %copy-start.2 = (f32[1024]{0:T(1024)S(1)}, f32[1024]{0:T(1024)}, u32[]{:S(2)}) copy-start(f32[1024]{0:T(1024)} %param.11) | copy-start | bytes 12292
  117.9 29.3 %all-to-all-start.2 = ((f32[64,24,128]{2,1,0:T(8,128)}), f32[64,24,128]{2,1,0:T(8,128)S(1)}, u32[]{:S(2)}, u32[]{:S(2)}) async-start(f32[64,24,128]{2,1,0:T(8,128)} %broadcast_in_dim.45), calls=%async_computation.2 | async-start | bytes 1572864 | tf_op jit(solution)/shard_map/all_to_all | solution.py:72
  196.3 5.2 %copy-start.1 = (bf16[1024,64]{0,1:T(8,128)(2,1)S(1)}, bf16[1024,64]{0,1:T(8,128)(2,1)}, u32[]{:S(2)}) copy-start(bf16[1024,64]{0,1:T(8,128)(2,1)} %param.8) | copy-start | bytes 393220
  196.3 60.7 %all-to-all-start.3 = ((bf16[8,512,1024]{2,1,0:T(8,128)(2,1)}), bf16[8,512,1024]{2,1,0:T(8,128)(2,1)}, u32[]{:S(2)}, u32[]{:S(2)}) async-start(bf16[8,512,1024]{2,1,0:T(8,128)(2,1)} %bitcast.67), calls=%async_computation.3 | async-start | bytes 16777216 | tf_op jit(solution)/shard_map/all_to_all | solution.py:47
  201.4 69.9 %collective-permute-start = (bf16[1024,1024]{1,0:T(8,128)(2,1)}, bf16[1024,1024]{1,0:T(8,128)(2,1)}, u32[]{:S(2)}, u32[]{:S(2)}) collective-permute-start(bf16[1024,1024]{1,0:T(8,128)(2,1)} %fusion.7), channel_id=1, source_target_pairs={{0,1},{1,0},{2,3},{3,2},{4,5},{5,4},{6,7},{7,6},{8,9},{9,8},{10,11... | collective-permute-start | bytes 6291464 | tf_op jit(solution)/shard_map/ppermute | solution.py:89
  207.5 62.6 %collective-permute-start.1 = (f32[64,4096]{1,0:T(8,128)S(1)}, f32[64,4096]{1,0:T(8,128)S(1)}, u32[]{:S(2)}, u32[]{:S(2)}) collective-permute-start(f32[64,4096]{1,0:T(8,128)S(1)} %convolution_bitcast_fusion), channel_id=1, source_target_pairs={{0,1},{1,0},{2,3},{3,2},{4,5},{5,4},{6,7},{7,6},{8,9},{9,8},{10,11... | collective-permute-start | bytes 3145736 | tf_op jit(solution)/shard_map/ppermute | solution.py:97
  263.6 17.8 %all-to-all-start.4 = ((bf16[8,64,1024]{2,1,0:T(8,128)(2,1)}), bf16[8,64,1024]{2,1,0:T(8,128)(2,1)S(1)}, u32[]{:S(2)}, u32[]{:S(2)}) async-start(bf16[8,64,1024]{2,1,0:T(8,128)(2,1)} %bitcast.14), calls=%async_computation.4 | async-start | bytes 2097152 | tf_op jit(solution)/shard_map/all_to_all | solution.py:47

commit v2 on v1

v2 whole, which is shorter than its diff:
```python
import jax
import jax.numpy as jnp
import numpy as np
from jax import lax
from jax.experimental import pallas as pl
from jax.experimental.pallas import tpu as pltpu
from jax.sharding import Mesh
from jax.sharding import PartitionSpec as P

TOK_DEV = 1024
HALVES = 2
VOCAB = ("vocab_0", "vocab_1", "vocab_2")
ALL = ("vocab_0", "vocab_1", "vocab_2", "dp")

ORDER = (((0, 1), (2, 3)), ((0, 3), (1, 2)))
SMALL = (((0, 1), (2, 3)), ((0, 3), (1, 2)))
LARGE = (((1, 2), (0, 3)), ((0, 1), (3, 2)))


def cubes(pairs):
    groups = []
    for core in (0, 1):
        for a in pairs[core]:
            for b in pairs[core]:
                for c in pairs[core]:
                    groups.append(
                        [((y * 4 + z) * 4 + x) * 2 + core for y in a for z in b for x in c]
                    )
    return groups


def steps_of(core):
    flat = [c for pair in ORDER[core] for c in pair]
    return [flat.index(c) // 2 for c in range(4)] + [flat.index(c) % 2 for c in range(4)]


SMALL_CUBES = cubes(SMALL)
LARGE_CUBES = cubes(LARGE)
STEPS = np.array([steps_of(0), steps_of(1)], np.int32)
SWAP = [(0, 1), (1, 0)]
F32 = jnp.float32
BF16 = jnp.bfloat16


def exchanged(x, groups):
    return lax.all_to_all(x, ALL, 0, 0, axis_index_groups=groups, tiled=True)


def to_cube(x, groups):
    return exchanged(jnp.broadcast_to(x[None], (8, *x.shape)), groups)


def place_of(steps, chip):
    y, z, x = chip // 16, (chip // 4) % 4, chip % 4
    large = (steps[y] * 2 + steps[z]) * 2 + steps[x]
    small = (steps[4 + y] * 2 + steps[4 + z]) * 2 + steps[4 + x]
    return large * 8 + small


def logits_kernel(steps, got, w, tgt, logits, stats, h, top, total, hit, sem):
    step = pl.program_id(0)
    rows, tokens = logits.shape

    @pl.when(step == 0)
    def _():
        def start(chip, carry):
            src = pl.multiple_of(place_of(steps, chip) * 64, 64)
            dst = pl.multiple_of(chip * 64, 64)
            pltpu.make_async_copy(got.at[pl.ds(src, 64)], h.at[pl.ds(dst, 64)], sem).start()
            return carry

        lax.fori_loop(0, 64, start, 0)
        top[...] = jnp.full(top.shape, -jnp.inf, F32)
        total[...] = jnp.zeros(total.shape, F32)
        hit[...] = jnp.zeros(hit.shape, F32)
        pltpu.make_async_copy(got, h, sem).wait()

    block = jnp.dot(w[...], h[...], preferred_element_type=F32)
    logits[...] = block
    at = lax.broadcasted_iota(jnp.int32, block.shape, 0) + step * rows
    hit[...] += jnp.sum(jnp.where(at == tgt[...], block, F32(0.0)), axis=0, keepdims=True)
    now = jnp.maximum(top[...], jnp.max(block, axis=0, keepdims=True))
    added = jnp.sum(jnp.exp(block - now), axis=0, keepdims=True)
    total[...] = total[...] * jnp.exp(top[...] - now) + added
    top[...] = now

    @pl.when(step == pl.num_programs(0) - 1)
    def _():
        lse = top[...] + jnp.log(total[...])
        both = [r[:, k : k + 128] for r in (lse, hit[...]) for k in range(0, tokens, 128)]
        stats[...] = jnp.broadcast_to(jnp.concatenate(both, axis=0)[None], stats.shape)


def logits_of(steps, got, w, tgt):
    vocab_rows, width = w.shape
    tokens = got.shape[1]
    rows = 256
    lines = 2 * tokens // 128
    return pl.pallas_call(
        logits_kernel,
        grid_spec=pltpu.PrefetchScalarGridSpec(
            num_scalar_prefetch=1,
            grid=(vocab_rows // rows,),
            in_specs=[
                pl.BlockSpec(memory_space=pl.ANY),
                pl.BlockSpec((rows, width), lambda i, s: (i, 0)),
                pl.BlockSpec((1, tokens), lambda i, s: (0, 0)),
            ],
            out_specs=[
                pl.BlockSpec((rows, tokens), lambda i, s: (i, 0)),
                pl.BlockSpec((64, lines, 128), lambda i, s: (0, 0, 0)),
            ],
            scratch_shapes=[
                pltpu.VMEM((width, tokens), BF16),
                pltpu.VMEM((1, tokens), F32),
                pltpu.VMEM((1, tokens), F32),
                pltpu.VMEM((1, tokens), F32),
                pltpu.SemaphoreType.DMA,
            ],
        ),
        out_shape=[
            jax.ShapeDtypeStruct((vocab_rows, tokens), F32),
            jax.ShapeDtypeStruct((64, lines, 128), F32),
        ],
        compiler_params=pltpu.CompilerParams(
            dimension_semantics=("arbitrary",), vmem_limit_bytes=48 << 20
        ),
        cost_estimate=pl.CostEstimate(
            flops=2 * vocab_rows * width * tokens,
            bytes_accessed=2 * width * (vocab_rows + tokens) + 4 * vocab_rows * tokens,
            transcendentals=vocab_rows * tokens,
        ),
    )(steps, got, w, tgt)


def grad_kernel(steps, stats, logits, cot, tgt, wt, part, grad, loss):
    step = pl.program_id(0)
    vocab_rows, tokens = logits.shape
    lines = tokens // 128

    @pl.when(step == 0)
    def _():
        lse = stats[:, :lines]
        top = jnp.max(lse, axis=0)
        full = top + jnp.log(jnp.sum(jnp.exp(lse - top[None]), axis=0))
        tok = full - jnp.sum(stats[:, lines:], axis=0)
        full = jnp.concatenate([full[k : k + 1] for k in range(lines)], axis=1)
        loss[...] = jnp.concatenate([tok[k : k + 1] for k in range(lines)], axis=1)
        for k in range(0, vocab_rows, 128):
            block = logits[k : k + 128, :]
            at = lax.broadcasted_iota(jnp.int32, block.shape, 0) + k
            one = jnp.where(at == tgt[...], F32(1.0), F32(0.0))
            grad[k : k + 128, :] = (cot[...] * (jnp.exp(block - full) - one)).astype(BF16)

    out = jnp.dot(wt[...], grad[...], preferred_element_type=F32).astype(BF16)
    for x in range(4):
        part[steps[x], steps[4 + x]] = out[64 * x : 64 * x + 64]


def grads_of(steps, stats, logits, cot, tgt, wt):
    width, vocab_rows = wt.shape
    tokens = logits.shape[1]
    whole = lambda *shape: pl.BlockSpec(shape, lambda i, s: (0,) * len(shape))
    part, grad, loss = pl.pallas_call(
        grad_kernel,
        grid_spec=pltpu.PrefetchScalarGridSpec(
            num_scalar_prefetch=1,
            grid=(16,),
            in_specs=[
                whole(*stats.shape),
                whole(vocab_rows, tokens),
                whole(1, tokens),
                whole(1, tokens),
                pl.BlockSpec((width // 16, vocab_rows), lambda i, s: (i, 0)),
            ],
            out_specs=[
                pl.BlockSpec(
                    (None, None, 2, None, None, 2, 64, tokens),
                    lambda i, s: (s[i // 4], s[i % 4], 0, s[4 + i // 4], s[4 + i % 4], 0, 0, 0),
                ),
                whole(vocab_rows, tokens),
                whole(1, tokens),
            ],
        ),
        out_shape=[
            jax.ShapeDtypeStruct((2, 2, 2, 2, 2, 2, 64, tokens), BF16),
            jax.ShapeDtypeStruct((vocab_rows, tokens), BF16),
            jax.ShapeDtypeStruct((1, tokens), F32),
        ],
        compiler_params=pltpu.CompilerParams(
            dimension_semantics=("arbitrary",), vmem_limit_bytes=48 << 20
        ),
        cost_estimate=pl.CostEstimate(
            flops=2 * vocab_rows * width * tokens,
            bytes_accessed=2 * width * (vocab_rows + tokens) + 6 * vocab_rows * tokens,
            transcendentals=vocab_rows * tokens,
        ),
    )(steps, stats, logits, cot, tgt, wt)
    return part.reshape(8, width // 8, tokens), grad, loss


def sum_kernel(pieces, out):
    out[...] = jnp.sum(pieces[...].astype(F32), axis=0).astype(BF16)


def summed(pieces):
    count, rows, tokens = pieces.shape
    step = min(rows, 64)
    return pl.pallas_call(
        sum_kernel,
        grid=(rows // step,),
        in_specs=[pl.BlockSpec((count, step, tokens), lambda i: (0, i, 0))],
        out_specs=pl.BlockSpec((step, tokens), lambda i: (i, 0)),
        out_shape=jax.ShapeDtypeStruct((rows, tokens), BF16),
        compiler_params=pltpu.CompilerParams(
            dimension_semantics=("arbitrary",), vmem_limit_bytes=16 << 20
        ),
        cost_estimate=pl.CostEstimate(
            flops=count * rows * tokens, bytes_accessed=2 * (count + 1) * rows * tokens,
            transcendentals=0,
        ),
    )(pieces)


def a_kernel(steps, own, *refs):
    *halves, out = refs
    done = None
    for k, half in enumerate(halves):
        tokens = half.shape[-1]
        block = jnp.concatenate([half[steps[x], steps[4 + x]] for x in range(4)], axis=0)
        now = lax.dot_general(
            own[:, k * tokens : (k + 1) * tokens], block, (((1,), (1,)), ((), ())),
            preferred_element_type=F32,
        )
        done = now if done is None else done + now
    out[...] = done


def a_part_of(steps, own, halves):
    feats, all_tokens = own.shape
    tokens = all_tokens // len(halves)
    width = halves[0].shape[0]
    half = pl.BlockSpec(
        (None, None, 2, None, None, 2, 64, tokens),
        lambda i, s: (s[i // 4], s[i % 4], 0, s[4 + i // 4], s[4 + i % 4], 0, 0, 0),
    )
    return pl.pallas_call(
        a_kernel,
        grid_spec=pltpu.PrefetchScalarGridSpec(
            num_scalar_prefetch=1,
            grid=(16,),
            in_specs=[pl.BlockSpec((feats, all_tokens), lambda i, s: (0, 0))] + [half] * len(halves),
            out_specs=pl.BlockSpec((feats, width // 16), lambda i, s: (0, i)),
        ),
        out_shape=jax.ShapeDtypeStruct((feats, width), F32),
        compiler_params=pltpu.CompilerParams(
            dimension_semantics=("arbitrary",), vmem_limit_bytes=16 << 20
        ),
        cost_estimate=pl.CostEstimate(
            flops=2 * feats * width * all_tokens, bytes_accessed=2 * width * all_tokens,
            transcendentals=0,
        ),
    )(steps, own, *[h.reshape(2, 2, 2, 2, 2, 2, 64, tokens) for h in halves])


def body(hidden, head_weight, targets, loss_cot):
    vocab_rows, width = head_weight.shape
    own = hidden.T
    feats, tokens = own.shape
    core = lax.axis_index("dp")
    steps = jnp.where(core == 0, jnp.asarray(STEPS[0]), jnp.asarray(STEPS[1]))
    some = to_cube(own, SMALL_CUBES).reshape(8 * feats, tokens)
    part_tokens = tokens // HALVES
    cuts = [slice(k * part_tokens, (k + 1) * part_tokens) for k in range(HALVES)]
    tgt = (targets - lax.axis_index(VOCAB) * vocab_rows)[None, :]
    cot = loss_cot[None, :]
    wt = head_weight.T
    gathered = [to_cube(some[:, c], LARGE_CUBES).reshape(width, part_tokens) for c in cuts]
    made = [logits_of(steps, g, head_weight, tgt[:, c]) for g, c in zip(gathered, cuts)]
    stats = [lax.all_to_all(s, VOCAB, 0, 0, tiled=True) for _, s in made]
    grads = [
        grads_of(steps, s, l, cot[:, c], tgt[:, c], wt) for s, (l, _), c in zip(stats, made, cuts)
    ]
    parts = [summed(exchanged(p, LARGE_CUBES)) for p, _, _ in grads]
    parts = [summed(exchanged(p.reshape(8, feats, part_tokens), SMALL_CUBES)) for p in parts]
    hidden_grad = jnp.concatenate(parts, axis=1).T
    tok_loss = jnp.concatenate([l[0] for _, _, l in grads])
    rows = vocab_rows // 2

    def gram(x):
        mine = lax.dynamic_slice_in_dim(x, core * rows, rows, 0)
        return lax.dot_general(mine, x, (((1,), (1,)), ((), ())), preferred_element_type=F32)

    mine = jnp.concatenate([g for _, g, _ in grads], axis=1)
    g_factor = (gram(mine) + gram(lax.ppermute(mine, "dp", SWAP))) / TOK_DEV
    a_part = a_part_of(steps, own, gathered)
    a_factor = (a_part + lax.ppermute(a_part, "dp", SWAP)) / TOK_DEV
    return (tok_loss, hidden_grad, g_factor, a_factor)


def solution(mesh):
    finer = Mesh(mesh.devices.reshape(4, 4, 4, mesh.shape["dp"]), ALL)
    return jax.shard_map(
        body,
        mesh=finer,
        in_specs=(P("dp", VOCAB), P(VOCAB, None), P("dp"), P("dp")),
        out_specs=(P("dp"), P("dp", VOCAB), P(ALL, None), P(VOCAB, None)),
        check_vma=False,
    )
```

time: 285 us -> 255 us (0.89)
  waiting for transfers between devices: 120 us -> 35.4 us
  Pallas kernels: 0 us -> 76.1 us
  blocking collectives: 16.2 us -> 54.5 us
  matrix products: 43.7 us -> 9.14 us
  other arithmetic: 30.8 us -> 2.35 us
  starting transfers between devices: 32.1 us -> 48.2 us
  local copies, waits for them, and re-layouts: 38.3 us -> 25.5 us
    pallas_call x0 -> x9, Pallas kernels: none -> 76.1 us  [the longest x2 31 us: grads_of(): pl.pallas_call(grad_kernel, grid_spec=pltpu.PrefetchScalarGridSpec(num_sc...]
    all_to_all x3 -> x5, waiting for transfers between devices: 104 us -> 35.4 us  [exchanged(): return lax.all_to_all(x, ALL, 0, 0, axis_index_groups=groups, tiled=True)]
    all_to_all x1 -> x2, blocking collectives: 16.2 us -> 54.5 us  [exchanged(): return lax.all_to_all(x, ALL, 0, 0, axis_index_groups=groups, tiled=True)]
    dot_general x3 -> x0, matrix products: 33.7 us -> none  [the longest x1 14.8 us: body(): lax.dot_general(head_weight, out_grad, (((0,), (0,)), ((), ())), preferre...]
    unnamed x12 -> x24, local copies, waits for them, and re-layouts: 1.93 us -> 20.7 us
    gather x2 -> x0, local copies, waits for them, and re-layouts: 17.8 us -> none  [the longest x1 8.91 us: body(): jnp.take(part.reshape(64, feats, tokens), jnp.asarray(CHIPS)[core], axis=0)]
    all_to_all x1 -> x2, waiting for transfers between devices: 16.4 us -> 0.01 us  [body(): stats = [lax.all_to_all(s, VOCAB, 0, 0, tiled=True) for _, s in made]]
    select_n x2 -> x1, other arithmetic: 14.9 us -> 0.01 us  [body(): steps = jnp.where(core == 0, jnp.asarray(STEPS[0]), jnp.asarray(STEPS[1]))]
  transfers between devices with their start and end apart: 6 -> 9, of which waited for: 4 -> 4; matrix products, arithmetic and copies ran while one was open for 9% -> 10% of each run, Pallas kernels for 0% -> 30%
where the time goes in v2:
time: 255 us; the launch traced here: 252 us
  Pallas kernels  76.1 us (30%)
  blocking collectives  54.5 us (21%)
  starting transfers between devices  48.2 us (19%)
  waiting for transfers between devices  35.4 us (14%)
  local copies, waits for them, and re-layouts  25.5 us (10%)
  matrix products  9.14 us (4%)
    all_to_all x2, blocking collectives, exchanged(): return lax.all_to_all(x, ALL, 0, 0, axis_index_groups=groups, tiled=True)  54.5 us
    all_to_all x5, waiting for transfers between devices, exchanged(): return lax.all_to_all(x, ALL, 0, 0, axis_index_groups=groups, tiled=True)  35.4 us
    pallas_call x2, Pallas kernels, grads_of(): pl.pallas_call(grad_kernel, grid_spec=pltpu.PrefetchScalarGridSpec(num_sc...  31 us
    all_to_all x5, starting transfers between devices, exchanged(): return lax.all_to_all(x, ALL, 0, 0, axis_index_groups=groups, tiled=True)  29.3 us
    pallas_call x2, Pallas kernels, logits_of(): pl.pallas_call(logits_kernel, grid_spec=pltpu.PrefetchScalarGridSpec(num_...  21.9 us
    unnamed x24, local copies, waits for them, and re-layouts  20.7 us
    all_to_all x2, starting transfers between devices, body(): stats = [lax.all_to_all(s, VOCAB, 0, 0, tiled=True) for _, s in made]  18.8 us
    pallas_call x4, Pallas kernels, summed(): pl.pallas_call(sum_kernel, grid=(rows // step,), in_specs=[pl.BlockSpec((...  11.9 us
  transfers between devices with their start and end apart: 9, of which 4 were waited for; matrix products, arithmetic and copies ran while one was open for 10% of the time, Pallas kernels for 30%

profile of v2, /device:TPU:0, one launch (start us, length us, event | category | flops | bytes accessed | tf_op | source)
XLA Modules:
  0.0 252.0 jit_solution(9171455502949425730)
XLA Ops:
  0.6 1.0 broadcast_in_dim.10
  1.7 16.2 %all_to_all.45 = bf16[8,64,1024]{2,1,0:T(8,128)(2,1)S(1)} all-to-all(bf16[8,64,1024]{2,1,0:T(8,128)(2,1)S(1)} %broadcast_in_dim.10), channel_id=1, replica_groups={{0,2,8,10,32,34,40,42},{4,6,12,14,36,38,44,46},{16,18,24,26,48,50,56,58..., dimensions={0} | all-to-all | bytes 2097152 | tf_op jit(solution)/shard_map/all_to_all | solution.py:46
  17.9 0.1 fusion.5
  18.0 0.4 broadcast_in_dim.28
  18.3 38.2 %all_to_all.46 = bf16[8,512,512]{2,1,0:T(8,128)(2,1)} all-to-all(bf16[8,512,512]{2,1,0:T(8,128)(2,1)S(1)} %broadcast_in_dim.28), channel_id=1, replica_groups={{42,44,50,52,74,76,82,84},{40,46,48,54,72,78,80,86},{34,36,58,60,66,68,..., dimensions={0} | all-to-all | bytes 8388608 | tf_op jit(solution)/shard_map/all_to_all | solution.py:46
  56.6 2.3 broadcast_in_dim.11
  58.9 4.6 %all-to-all-start.1 = ((bf16[8,512,512]{2,1,0:T(8,128)(2,1)}), bf16[8,512,512]{2,1,0:T(8,128)(2,1)}, u32[]{:S(2)}, u32[]{:S(2)}) async-start(bf16[8,512,512]{2,1,0:T(8,128)(2,1)} %broadcast_in_dim.11), calls=%async_computation.1 | async-start | bytes 8388608 | tf_op jit(solution)/shard_map/all_to_all | solution.py:46
  63.5 0.0 copy-start.8
  63.5 0.0 copy-start.9
  63.5 0.0 copy-start.6
  63.5 0.0 copy-start.7
  63.5 12.0 %copy.10 = bf16[1024,4096]{0,1:T(8,128)(2,1)} copy(bf16[1024,4096]{1,0:T(8,128)(2,1)} %w.3) | data formatting | bytes 16777216 | tf_op args[1]
  75.6 10.9 %shard_map.95 = (f32[1024,512]{1,0:T(8,128)S(1)}, f32[64,8,128]{2,1,0:T(8,128)}) custom-call(s32[8]{0:T(128)S(1)} %broadcast_select_fusion.steps, bf16[4096,512]{1,0:T(8,128)(2,1)} %bitcast.19, bf16[1024,4096]{1,0:T(8,128)(2,1)} %w.3, s32[1,512]{1,0:T(1,128)S(1)} %get-tuple-element.29.tgt), custom_call_target="tpu_custom_call" | custom-call | flops 4294967296 | bytes 14680064 | tf_op jit(solution)/shard_map/pallas_call | solution.py:99
  86.6 0.0 copy-start.4
  86.6 1.3 copy-done.4
  87.9 7.3 %all-to-all-done.1 = bf16[8,512,512]{2,1,0:T(8,128)(2,1)} async-done(((bf16[8,512,512]{2,1,0:T(8,128)(2,1)}), bf16[8,512,512]{2,1,0:T(8,128)(2,1)}, u32[]{:S(2)}, u32[]{:S(2)}) %all-to-all-start.1) | async-done | bytes 4194336 | tf_op jit(solution)/shard_map/all_to_all | solution.py:46
  95.2 8.4 %all-to-all-start.4 = ((f32[64,8,128]{2,1,0:T(8,128)}), f32[64,8,128]{2,1,0:T(8,128)S(1)}, u32[]{:S(2)}, u32[]{:S(2)}) async-start(f32[64,8,128]{2,1,0:T(8,128)} %get-tuple-element.17), calls=%async_computation.4 | async-start | bytes 524288 | tf_op jit(solution)/shard_map/all_to_all | solution.py:280
  103.6 10.9 %shard_map.93 = (f32[1024,512]{1,0:T(8,128)S(1)}, f32[64,8,128]{2,1,0:T(8,128)}) custom-call(s32[8]{0:T(128)S(1)} %broadcast_select_fusion.steps, bf16[4096,512]{1,0:T(8,128)(2,1)} %bitcast.2.got, bf16[1024,4096]{1,0:T(8,128)(2,1)} %w.3, s32[1,512]{1,0:T(1,128)S(1)} %get-tuple-element.28.tgt), custom_call_target="tpu_custom_call" | custom-call | flops 4294967296 | bytes 14680064 | tf_op jit(solution)/shard_map/pallas_call | solution.py:99
  114.6 1.4 copy-done.2
  116.0 0.0 all-to-all-done.4.stats
  116.0 10.3 %all-to-all-start.2 = ((f32[64,8,128]{2,1,0:T(8,128)}), f32[64,8,128]{2,1,0:T(8,128)S(1)}, u32[]{:S(2)}, u32[]{:S(2)}) async-start(f32[64,8,128]{2,1,0:T(8,128)} %get-tuple-element.14), calls=%async_computation.2 | async-start | bytes 524288 | tf_op jit(solution)/shard_map/all_to_all | solution.py:280
  126.3 0.0 copy-start.5
  126.3 1.6 copy-done.5
  127.9 15.5 %shard_map.96 = (bf16[2,2,2,2,2,2,64,512]{7,6,5,4,3,2,1,0:T(8,128)(2,1)}, bf16[1024,512]{1,0:T(8,128)(2,1)S(1)}, f32[1,512]{1,0:T(1,128)S(1)}) custom-call(s32[8]{0:T(128)S(1)} %broadcast_select_fusion.steps, f32[64,8,128]{2,1,0:T(8,128)S(1)} %all-to-all-done.4.stats, f32[1024,512]{1,0:T(8,128)S(1)} %copy-done.5, f32[1,512]{1,0:T(1,128)S(1)} %get-tuple-element.27.cot, ...), custom_call_target="tpu_custom_call" | custom-call | flops 4294967296 | bytes 15728640 | tf_op jit(solution)/shard_map/pallas_call | solution.py:164
  143.4 8.6 %all-to-all-start.7 = ((bf16[8,512,512]{2,1,0:T(8,128)(2,1)}), bf16[8,512,512]{2,1,0:T(8,128)(2,1)}, u32[]{:S(2)}, u32[]{:S(2)}) async-start(bf16[8,512,512]{2,1,0:T(8,128)(2,1)} %bitcast.28), calls=%async_computation.7 | async-start | bytes 8388608 | tf_op jit(solution)/shard_map/all_to_all | solution.py:46
  152.0 1.6 copy-done.3
  153.6 15.5 %shard_map.94 = (bf16[2,2,2,2,2,2,64,512]{7,6,5,4,3,2,1,0:T(8,128)(2,1)}, bf16[1024,512]{1,0:T(8,128)(2,1)S(1)}, f32[1,512]{1,0:T(1,128)S(1)}) custom-call(s32[8]{0:T(128)S(1)} %broadcast_select_fusion.steps, f32[64,8,128]{2,1,0:T(8,128)S(1)} %all-to-all-done.2.stats, f32[1024,512]{1,0:T(8,128)S(1)} %copy-done.3, f32[1,512]{1,0:T(1,128)S(1)} %get-tuple-element.26.cot, ...), custom_call_target="tpu_custom_call" | custom-call | flops 4294967296 | bytes 15728640 | tf_op jit(solution)/shard_map/pallas_call | solution.py:164
  169.1 14.7 %all-to-all-done.7.pieces = bf16[8,512,512]{2,1,0:T(8,128)(2,1)} async-done(((bf16[8,512,512]{2,1,0:T(8,128)(2,1)}), bf16[8,512,512]{2,1,0:T(8,128)(2,1)}, u32[]{:S(2)}, u32[]{:S(2)}) %all-to-all-start.7) | async-done | bytes 4194336 | tf_op jit(solution)/shard_map/all_to_all | solution.py:46
  183.8 7.6 %all-to-all-start.5 = ((bf16[8,512,512]{2,1,0:T(8,128)(2,1)}), bf16[8,512,512]{2,1,0:T(8,128)(2,1)}, u32[]{:S(2)}, u32[]{:S(2)}) async-start(bf16[8,512,512]{2,1,0:T(8,128)(2,1)} %bitcast.27), calls=%async_computation.5 | async-start | bytes 8388608 | tf_op jit(solution)/shard_map/all_to_all | solution.py:46
  191.4 1.0 constant_dynamic-update-slice_fusion.1
  192.5 1.0 constant_dynamic-update-slice_fusion
  193.5 0.9 copy-done
  194.4 11.3 %shard_map.101 = f32[64,4096]{1,0:T(8,128)S(1)} custom-call(s32[8]{0:T(128)S(1)} %broadcast_select_fusion.steps, bf16[64,1024]{1,0:T(8,128)(2,1)S(1)} %bitcast.22, bf16[2,2,2,2,2,2,64,512]{7,6,5,4,3,2,1,0:T(8,128)(2,1)} %bitcast.14.refs_0_, bf16[2,2,2,2,2,2,64,512]{7,6,5,4,3,2,1,0:T(8,128)(2,1)S(1)} %bitcast.20), custom_call_target="tpu_custom_call" | custom-call | flops 536870912 | bytes 8388608 | tf_op jit(solution)/shard_map/pallas_call | solution.py:247
  205.7 0.1 collective-permute-start.1
  205.8 5.9 %shard_map.99 = bf16[512,512]{1,0:T(8,128)(2,1)} custom-call(bf16[8,512,512]{2,1,0:T(8,128)(2,1)} %all-to-all-done.7.pieces), custom_call_target="tpu_custom_call" | custom-call | flops 2097152 | bytes 4718592 | tf_op jit(solution)/shard_map/pallas_call | solution.py:209
  211.7 11.5 %all-to-all-done.5.pieces = bf16[8,512,512]{2,1,0:T(8,128)(2,1)} async-done(((bf16[8,512,512]{2,1,0:T(8,128)(2,1)}), bf16[8,512,512]{2,1,0:T(8,128)(2,1)}, u32[]{:S(2)}, u32[]{:S(2)}) %all-to-all-start.5) | async-done | bytes 4194336 | tf_op jit(solution)/shard_map/all_to_all | solution.py:46
  223.2 3.5 %all-to-all-start.8 = ((bf16[8,64,512]{2,1,0:T(8,128)(2,1)}), bf16[8,64,512]{2,1,0:T(8,128)(2,1)S(1)}, u32[]{:S(2)}, u32[]{:S(2)}) async-start(bf16[8,64,512]{2,1,0:T(8,128)(2,1)} %bitcast.12), calls=%async_computation.8 | async-start | bytes 1048576 | tf_op jit(solution)/shard_map/all_to_all | solution.py:46
  226.7 0.6 pad_maximum_fusion
  227.3 4.6 %fusion.1 = f32[512,1024]{1,0:T(8,128)} fusion(bf16[1024,1024]{1,0:T(8,128)(2,1)} %constant_dynamic-update-slice_fusion, s32[]{:T(128)S(6)} %select_n.14), kind=kOutput, calls=%fused_computation.3 | convolution fusion | flops 1073741824 | bytes 5242884 | tf_op jit(solution)/shard_map/dot_general | solution.py:292
  231.9 5.9 %shard_map.97 = bf16[512,512]{1,0:T(8,128)(2,1)} custom-call(bf16[8,512,512]{2,1,0:T(8,128)(2,1)} %all-to-all-done.5.pieces), custom_call_target="tpu_custom_call" | custom-call | flops 2097152 | bytes 4718592 | tf_op jit(solution)/shard_map/pallas_call | solution.py:209
  237.8 5.0 %all-to-all-start.6 = ((bf16[8,64,512]{2,1,0:T(8,128)(2,1)}), bf16[8,64,512]{2,1,0:T(8,128)(2,1)S(1)}, u32[]{:S(2)}, u32[]{:S(2)}) async-start(bf16[8,64,512]{2,1,0:T(8,128)(2,1)} %bitcast.10), calls=%async_computation.6 | async-start | bytes 1048576 | tf_op jit(solution)/shard_map/all_to_all | solution.py:46
  242.9 1.1 add_multiply_fusion.1
  244.0 0.9 copy-done.10
  244.8 4.5 %add_multiply_fusion = f32[512,1024]{1,0:T(8,128)} fusion(f32[512,1024]{1,0:T(8,128)S(1)} %copy-done.10, bf16[1024,1024]{1,0:T(8,128)(2,1)} %collective-permute-done, s32[]{:T(128)S(6)} %select_n.14), kind=kOutput, calls=%fused_computation | convolution fusion | flops 1074790400 | bytes 7340036 | tf_op jit(solution)/shard_map/dot_general | solution.py:292
  249.4 0.1 shard_map.100
  249.4 1.8 all-to-all-done.6.pieces
  251.2 0.1 shard_map.98
  251.3 0.7 maximum_bitcast_fusion
  (19 shorter events, 0.0 us)
Async XLA Ops:
  58.9 36.3 %all-to-all-start.1 = ((bf16[8,512,512]{2,1,0:T(8,128)(2,1)}), bf16[8,512,512]{2,1,0:T(8,128)(2,1)}, u32[]{:S(2)}, u32[]{:S(2)}) async-start(bf16[8,512,512]{2,1,0:T(8,128)(2,1)} %broadcast_in_dim.11), calls=%async_computation.1 | async-start | bytes 8388608 | tf_op jit(solution)/shard_map/all_to_all | solution.py:46
  63.5 12.1 %copy-start.8 = (s32[8]{0:T(128)S(1)}, s32[8]{0:T(128)}, u32[]{:S(2)}) copy-start(s32[8]{0:T(128)} %constant.35.clone) | copy-start | bytes 100
  63.5 12.1 %copy-start.9 = (s32[8]{0:T(128)S(1)}, s32[8]{0:T(128)}, u32[]{:S(2)}) copy-start(s32[8]{0:T(128)} %constant.34.clone) | copy-start | bytes 100
  63.5 12.1 %copy-start.6 = (s32[1024]{0:T(1024)S(1)}, s32[1024]{0:T(1024)}, u32[]{:S(2)}) copy-start(s32[1024]{0:T(1024)} %param.8) | copy-start | bytes 12292
  63.5 12.1 %copy-start.7 = (f32[1024]{0:T(1024)S(1)}, f32[1024]{0:T(1024)}, u32[]{:S(2)}) copy-start(f32[1024]{0:T(1024)} %param.9) | copy-start | bytes 12292
  86.6 1.3 copy-start.4
  95.2 20.8 %all-to-all-start.4 = ((f32[64,8,128]{2,1,0:T(8,128)}), f32[64,8,128]{2,1,0:T(8,128)S(1)}, u32[]{:S(2)}, u32[]{:S(2)}) async-start(f32[64,8,128]{2,1,0:T(8,128)} %get-tuple-element.17), calls=%async_computation.4 | async-start | bytes 524288 | tf_op jit(solution)/shard_map/all_to_all | solution.py:280
  114.6 1.4 copy-start.2
  116.0 27.4 %all-to-all-start.2 = ((f32[64,8,128]{2,1,0:T(8,128)}), f32[64,8,128]{2,1,0:T(8,128)S(1)}, u32[]{:S(2)}, u32[]{:S(2)}) async-start(f32[64,8,128]{2,1,0:T(8,128)} %get-tuple-element.14), calls=%async_computation.2 | async-start | bytes 524288 | tf_op jit(solution)/shard_map/all_to_all | solution.py:280
  126.3 1.6 copy-start.5
  143.4 40.4 %all-to-all-start.7 = ((bf16[8,512,512]{2,1,0:T(8,128)(2,1)}), bf16[8,512,512]{2,1,0:T(8,128)(2,1)}, u32[]{:S(2)}, u32[]{:S(2)}) async-start(bf16[8,512,512]{2,1,0:T(8,128)(2,1)} %bitcast.28), calls=%async_computation.7 | async-start | bytes 8388608 | tf_op jit(solution)/shard_map/all_to_all | solution.py:46
  152.0 1.6 copy-start.3
  183.8 9.7 %copy-start.1 = (bf16[1024,64]{0,1:T(8,128)(2,1)S(1)}, bf16[1024,64]{0,1:T(8,128)(2,1)}, u32[]{:S(2)}) copy-start(bf16[1024,64]{0,1:T(8,128)(2,1)} %param.6) | copy-start | bytes 393220
  183.8 39.4 %all-to-all-start.5 = ((bf16[8,512,512]{2,1,0:T(8,128)(2,1)}), bf16[8,512,512]{2,1,0:T(8,128)(2,1)}, u32[]{:S(2)}, u32[]{:S(2)}) async-start(bf16[8,512,512]{2,1,0:T(8,128)(2,1)} %bitcast.27), calls=%async_computation.5 | async-start | bytes 8388608 | tf_op jit(solution)/shard_map/all_to_all | solution.py:46
  191.4 2.9 %copy-start = (bf16[8,512,512]{2,1,0:T(8,128)(2,1)S(1)}, bf16[8,512,512]{2,1,0:T(8,128)(2,1)}, u32[]{:S(2)}) copy-start(bf16[8,512,512]{2,1,0:T(8,128)(2,1)} %all_to_all.46) | copy-start | bytes 12582916
  193.5 50.5 %collective-permute-start = (bf16[1024,1024]{1,0:T(8,128)(2,1)}, bf16[1024,1024]{1,0:T(8,128)(2,1)}, u32[]{:S(2)}, u32[]{:S(2)}) collective-permute-start(bf16[1024,1024]{1,0:T(8,128)(2,1)} %constant_dynamic-update-slice_fusion), channel_id=1, source_target_pairs={{0,1},{1,0},{2,3},{3,2},{4,5},{5,4},{6,7},{7,6},{8,9},{9,8},{10,11... | collective-permute-start | bytes 6291464 | tf_op jit(solution)/shard_map/ppermute | solution.py:295
  205.7 37.2 %collective-permute-start.1 = (f32[64,4096]{1,0:T(8,128)S(1)}, f32[64,4096]{1,0:T(8,128)S(1)}, u32[]{:S(2)}, u32[]{:S(2)}) collective-permute-start(f32[64,4096]{1,0:T(8,128)S(1)} %shard_map.101), channel_id=1, source_target_pairs={{0,1},{1,0},{2,3},{3,2},{4,5},{5,4},{6,7},{7,6},{8,9},{9,8},{10,11... | collective-permute-start | bytes 3145736 | tf_op jit(solution)/shard_map/ppermute | solution.py:297
  223.2 14.6 %all-to-all-start.8 = ((bf16[8,64,512]{2,1,0:T(8,128)(2,1)}), bf16[8,64,512]{2,1,0:T(8,128)(2,1)S(1)}, u32[]{:S(2)}, u32[]{:S(2)}) async-start(bf16[8,64,512]{2,1,0:T(8,128)(2,1)} %bitcast.12), calls=%async_computation.8 | async-start | bytes 1048576 | tf_op jit(solution)/shard_map/all_to_all | solution.py:46
  237.8 13.4 %all-to-all-start.6 = ((bf16[8,64,512]{2,1,0:T(8,128)(2,1)}), bf16[8,64,512]{2,1,0:T(8,128)(2,1)S(1)}, u32[]{:S(2)}, u32[]{:S(2)}) async-start(bf16[8,64,512]{2,1,0:T(8,128)(2,1)} %bitcast.10), calls=%async_computation.6 | async-start | bytes 1048576 | tf_op jit(solution)/shard_map/all_to_all | solution.py:46
  242.9 2.0 copy-start.10
